TPU v7x, 128 devices: a whole 4x4x4 slice. The times are simulated.
128 devices in a mesh: point: 32 (over z_hi, x, y), batch: 4 (over z_lo, core).
Axes of the slice: x: 4, y: 4, z: 4 (z_hi: 2, z_lo: 2; z = z_hi * 2 + z_lo), core: 2. Of those that a mesh axis runs over, the one named last changes fastest.
Arguments:
- activations: bfloat16 [128, 14, 14, 1024], P('batch'), may hold values from -8 to 8
- labels: int32 [128], P('batch'), may hold values from 0 to 999
- t_values: float32 [64], replicated, may hold values from 0 to 1
- point_index: int32 [32], replicated, may hold values from 0 to 63
- w_reduce: bfloat16 [3, 1024, 256], P(None, 'point'), may hold values from -1 to 1
- w_spatial: bfloat16 [3, 2304, 256], P(None, 'point'), may hold values from -0.125 to 0.125
- w_expand: bfloat16 [3, 256, 1024], P(None, 'point'), may hold values from -0.375 to 0.375
- w_classes: bfloat16 [3, 1000, 1024], P(None, None, 'point'), may hold values from -0.1875 to 0.1875
- norm_gain: float32 [3, 1536], replicated, may hold values from 0.5 to 1.5
- norm_bias: float32 [3, 1536], replicated, may hold values from -3 to 3
- class_bias: float32 [3, 1000], replicated, may hold values from -3 to 3
Outputs:
- mean_reduce: float32 [32, 256], P('point')
- var_reduce: float32 [32, 256], P('point')
- mean_spatial: float32 [32, 256], P('point')
- var_spatial: float32 [32, 256], P('point')
- mean_expand: float32 [32, 1024], P('point')
- var_expand: float32 [32, 1024], P('point')
- margin: float32 [32], replicated
All inputs are finite; a program needn't handle non-finite values.
Results may differ from a plain program's by a relative error of at most 0.003.
Values may be sent and summed in bfloat16 or wider, within the bound.
No kernel may reach another device: no remote copies, remote signals or barrier semaphores. Data moves between devices by JAX's collectives and lax.ppermute only.
A program may use at most 128 MiB of HBM per device.

v0:
```python
import jax
import jax.numpy as jnp
from jax import lax
from jax.sharding import Mesh
from jax.sharding import PartitionSpec as P

BATCH = ("batch_0", "batch_1")
EPSILON = 1e-05


def by_axis(x, axes):
    for axis in axes:
        x = lax.psum(x, axis)
    return x


def sent_to_all(x, axis):
    copies = jnp.broadcast_to(x, (lax.axis_size(axis), *x.shape))
    return lax.all_to_all(copies, axis, split_axis=0, concat_axis=0, tiled=True)


def over_copies(x, axis):
    everything = sent_to_all(x, axis)
    return jnp.sum(everything, axis=0)


def joined_along(blocks, dim):
    blocks = jnp.moveaxis(blocks, 0, dim)
    dims = blocks.shape
    return blocks.reshape(*dims[:dim], dims[dim] * dims[dim + 1], *dims[dim + 2 :])


def gather_directly(x, axis, dim):
    blocks = sent_to_all(x, axis)
    return joined_along(blocks, dim)


def curve_coefficients(t_values, point_index):
    table_size = t_values.shape[0]
    matches = point_index[:, None] == jnp.arange(table_size, dtype=jnp.int32)[None, :]
    picked = jnp.sum(jnp.where(matches, t_values[None, :], 0.0), axis=1)
    doubled = 2.0 * picked
    return jnp.stack(
        [
            jnp.maximum(1.0 - doubled, 0.0),
            1.0 - jnp.abs(1.0 - doubled),
            jnp.maximum(doubled - 1.0, 0.0),
        ],
        axis=1,
    )


def blend_all(coefficients, endpoints):
    target_shape = (coefficients.shape[0],) + (1,) * (endpoints.ndim - 1)
    start_part = coefficients[:, 0].reshape(target_shape) * endpoints[0].astype(jnp.float32)[None]
    bend_part = coefficients[:, 1].reshape(target_shape) * endpoints[1].astype(jnp.float32)[None]
    final_part = coefficients[:, 2].reshape(target_shape) * endpoints[2].astype(jnp.float32)[None]
    return start_part + bend_part + final_part


def point_weight(endpoints, coefficients, by_columns):
    all_points = blend_all(coefficients, endpoints).astype(jnp.bfloat16)
    if by_columns:
        received = lax.all_to_all(all_points, "point", split_axis=0, concat_axis=2, tiled=True)
    else:
        received = lax.all_to_all(all_points, "point", split_axis=0, concat_axis=1, tiled=True)
    return received[0]


def map_product(maps, kernel):
    return lax.dot_general(
        maps, kernel, (((3,), (0,)), ((), ())), preferred_element_type=jnp.float32
    )


def batch_norm(pre_norm, gain_part, bias_part, row_count):
    channel_total, channel_squares = (
        by_axis(jnp.sum(pre_norm, axis=(0, 1, 2)), BATCH),
        by_axis(jnp.sum(pre_norm * pre_norm, axis=(0, 1, 2)), BATCH),
    )
    channel_mean = channel_total / row_count
    channel_var = channel_squares / row_count - channel_mean * channel_mean
    scaled = (pre_norm - channel_mean) * lax.rsqrt(channel_var + EPSILON) * gain_part + bias_part
    return (channel_mean, channel_var, scaled)


def spatial_conv(source, kernel):
    side_len = source.shape[1]
    middle = source.shape[3]
    padded = jnp.pad(source, ((0, 0), (1, 1), (1, 1), (0, 0)))
    widened = jnp.concatenate(
        [
            padded[:, :, 0:side_len, :],
            padded[:, :, 1 : side_len + 1, :],
            padded[:, :, 2 : side_len + 2, :],
        ],
        axis=3,
    )
    summed = map_product(widened[:, 0:side_len], kernel[0 : 3 * middle])
    summed = summed + map_product(widened[:, 1 : side_len + 1], kernel[3 * middle : 6 * middle])
    summed = summed + map_product(widened[:, 2 : side_len + 2], kernel[6 * middle : 9 * middle])
    return summed


def shards(
    activations,
    labels,
    t_values,
    point_index,
    w_reduce,
    w_spatial,
    w_expand,
    w_classes,
    norm_gain,
    norm_bias,
    class_bias,
):
    coefficients = curve_coefficients(t_values, point_index)
    own_row = lax.dynamic_slice_in_dim(coefficients, lax.axis_index("point"), 1, 0)
    reduce_w = point_weight(w_reduce, coefficients, False)
    spatial_w = point_weight(w_spatial, coefficients, False)
    expand_w = point_weight(w_expand, coefficients, False)
    class_w = point_weight(w_classes, coefficients, True)
    gain_now = blend_all(own_row, norm_gain)[0]
    bias_now = blend_all(own_row, norm_bias)[0]
    shift_now = blend_all(own_row, class_bias)[0]
    images, side_len, _, channels = activations.shape
    middle = w_reduce.shape[2]
    row_count = float(images * side_len * side_len * lax.axis_size(BATCH))
    reduced = map_product(activations, reduce_w)
    mean_one, var_one, normed_one = batch_norm(
        reduced, gain_now[:middle], bias_now[:middle], row_count
    )
    first = jax.nn.relu(normed_one).astype(jnp.bfloat16)
    spatial = spatial_conv(first, spatial_w)
    mean_two, var_two, normed_two = batch_norm(
        spatial, gain_now[middle : 2 * middle], bias_now[middle : 2 * middle], row_count
    )
    second = jax.nn.relu(normed_two).astype(jnp.bfloat16)
    expanded = map_product(second, expand_w)
    mean_three, var_three, normed_three = batch_norm(
        expanded, gain_now[2 * middle :], bias_now[2 * middle :], row_count
    )
    block_out = jax.nn.relu(normed_three + activations.astype(jnp.float32))
    pooled = jnp.mean(block_out, axis=(1, 2)).astype(jnp.bfloat16)
    logits = (
        lax.dot_general(
            pooled, class_w, (((1,), (1,)), ((), ())), preferred_element_type=jnp.float32
        )
        + shift_now
    )
    classes = logits.shape[1]
    onehot = labels[:, None] == jnp.arange(classes, dtype=jnp.int32)[None, :]
    correct = jnp.sum(jnp.where(onehot, logits, 0.0), axis=1)
    rivals = jnp.max(jnp.where(onehot, -1e30, logits), axis=1)
    partial_value = jnp.sum(correct - rivals) / (images * lax.axis_size(BATCH))
    group_sum = over_copies(partial_value.reshape(1), BATCH)
    margin_all = gather_directly(group_sum, "point", 0)
    return (
        mean_one[None],
        var_one[None],
        mean_two[None],
        var_two[None],
        mean_three[None],
        var_three[None],
        margin_all,
    )


def solution(mesh):
    torus = Mesh(mesh.devices.reshape(mesh.shape["point"], 2, 2), ("point", "batch_0", "batch_1"))
    return jax.shard_map(
        shards,
        mesh=torus,
        in_specs=(
            P(BATCH, None, None, None),
            P(BATCH),
            P(),
            P(),
            P(None, "point", None),
            P(None, "point", None),
            P(None, "point", None),
            P(None, None, "point"),
            P(),
            P(),
            P(),
        ),
        out_specs=(
            P("point", None),
            P("point", None),
            P("point", None),
            P("point", None),
            P("point", None),
            P("point", None),
            P(),
        ),
        check_vma=False,
    )
```

profile of v0, /device:TPU:0, one launch (start us, length us, event | category | flops | bytes accessed | tf_op | source)
XLA Modules:
  0.0 189.2 jit_solution(16724359364042612514)
XLA Ops:
  3.3 10.7 %all-to-all-start = ((bf16[32,32,256]{2,1,0:T(8,128)(2,1)}), bf16[32,32,256]{2,1,0:T(8,128)(2,1)S(1)}, u32[]{:S(2)}, u32[]{:S(2)}) async-start(bf16[32,32,256]{2,1,0:T(8,128)(2,1)} %add_convert_fusion.3), calls=%async_computation | async-start | bytes 1048576 | tf_op jit(solution)/shard_map/all_to_all | solution.py:66
  14.7 2.8 %multiply_add_fusion = (f32[1,1536]{1,0:T(1,128)S(1)}, f32[1,1536]{1,0:T(1,128)S(1)}) fusion(f32[3,1536]{1,0:T(4,128)} %param.20, f32[]{:T(128)} %bitcast.13, f32[]{:T(128)} %bitcast.12, f32[]{:T(128)} %bitcast.11, f32[3,1536]{1,0:T(4,128)} %param.19), kind=kLoop, calls=%fused_computation.48 | loop fusion | flops 15360 | bytes 49164 | tf_op jit(solution)/shard_map/add | solution.py:58
  19.1 2.8 %multiply_add_fusion.2 = f32[1,1000]{1,0:T(1,128)S(1)} fusion(f32[3,1000]{1,0:T(4,128)} %param.21, f32[]{:T(128)} %bitcast.13, f32[]{:T(128)} %bitcast.12, f32[]{:T(128)} %bitcast.11), kind=kLoop, calls=%fused_computation.50 | loop fusion | flops 5000 | bytes 16012 | tf_op jit(solution)/shard_map/add | solution.py:58
  22.9 1.6 add_convert_fusion.1
  25.6 2.4 %add_convert_fusion = bf16[32,1000,32]{1,2,0:T(8,128)(2,1)} fusion(f32[1000,32]{0,1:T(8,128)S(1)} %get-tuple-element.37, f32[32]{0:T(128)S(1)} %get-tuple-element.60, f32[1000,32]{0,1:T(8,128)S(1)} %get-tuple-element.38, f32[32]{0:T(128)S(1)} %get-tuple-element.61, f32[1000,32]{0,1:T(8,128)S(1)} %get-tuple-element.36, f32[32]{0:T(128)S(1)} %get-tuple-element.62), kind=kLoop, calls=%fused_computation.8 | loop fusion | flops 6144000 | bytes 2432384 | tf_op jit(solution)/shard_map/convert_element_type | solution.py:62
  27.9 9.8 %all-to-all-start.1 = ((bf16[32,72,256]{2,1,0:T(8,128)(2,1)}), bf16[32,72,256]{2,1,0:T(8,128)(2,1)S(1)}, u32[]{:S(2)}, u32[]{:S(2)}) async-start(bf16[32,72,256]{2,1,0:T(8,128)(2,1)} %add_convert_fusion.1), calls=%async_computation.1 | async-start | bytes 2359296 | tf_op jit(solution)/shard_map/all_to_all | solution.py:66
  37.8 10.8 %multiply_reduce_fusion.2 = (f32[256]{0:T(256)S(1)}, f32[256]{0:T(256)S(1)}, f32[256,32,14,14]{0,1,3,2:T(8,128)}) fusion(bf16[1024,256,1,1]{1,0,3,2:T(8,128)(2,1)S(1)} %bitcast.103, bf16[32,14,14,1024]{3,0,2,1:T(8,128)(2,1)} %param.11), kind=kOutput, calls=%fused_computation.7 | convolution fusion | flops 3293150720 | bytes 19793920 | tf_op jit(solution)/shard_map/dot_general | solution.py:71
  48.6 5.1 %all-reduce.6 = (f32[256]{0:T(256)S(1)}, f32[256]{0:T(256)S(1)}) all-reduce(f32[256]{0:T(256)S(1)} %get-tuple-element.12, f32[256]{0:T(256)S(1)} %get-tuple-element.11), channel_id=1, replica_groups=mesh['point'=32,'batch_0'=2,'batch_1'=2] {'batch_0'}, use_global_device_ids=true, to_apply=%region_2.3 | all-reduce | flops 512 | bytes 4096 | tf_op jit(solution)/shard_map/psum | solution.py:13
  53.8 2.4 %all-reduce.3 = (f32[256]{0:T(256)S(1)}, f32[256]{0:T(256)S(1)}) all-reduce(f32[256]{0:T(256)S(1)} %get-tuple-element.25, f32[256]{0:T(256)S(1)} %get-tuple-element.26), channel_id=1, replica_groups=mesh['point'=32,'batch_0'=2,'batch_1'=2] {'batch_1'}, use_global_device_ids=true, to_apply=%region_3.4 | all-reduce | flops 512 | bytes 4096 | tf_op jit(solution)/shard_map/psum | solution.py:13
  56.8 4.1 %fusion.1 = bf16[32,14,14,256]{3,0,2,1:T(8,128)(2,1)S(1)} fusion(f32[256,32,14,14]{0,1,3,2:T(8,128)} %get-tuple-element.63, f32[256]{0:T(256)S(1)} %bitcast.110, f32[256]{0:T(256)S(1)} %bitcast.111, f32[256]{0:T(256)S(1)} %get-tuple-element.31, f32[256]{0:T(256)S(1)} %get-tuple-element.57), kind=kLoop, calls=%fused_computation.13 | loop fusion | flops 9633792 | bytes 9637888 | tf_op jit(solution)/shard_map/convert_element_type | solution.py:134
  60.8 4.9 %pad_slice_fusion.2 = (bf16[32,16,14,256]{3,0,2,1:T(8,128)(2,1)}, bf16[32,16,14,256]{3,0,2,1:T(8,128)(2,1)}, bf16[32,16,14,256]{3,0,2,1:T(8,128)(2,1)}) fusion(bf16[32,14,14,256]{3,0,2,1:T(8,128)(2,1)S(1)} %fusion.1), kind=kLoop, calls=%fused_computation.11 | loop fusion | bytes 14221312 | tf_op jit(solution)/shard_map/slice | solution.py:93
  65.8 9.8 %all-to-all-start.2 = ((bf16[32,8,1024]{2,1,0:T(8,128)(2,1)}), bf16[32,8,1024]{2,1,0:T(8,128)(2,1)S(1)}, u32[]{:S(2)}, u32[]{:S(2)}) async-start(bf16[32,8,1024]{2,1,0:T(8,128)(2,1)} %add_convert_fusion.2), calls=%async_computation.2 | async-start | bytes 1048576 | tf_op jit(solution)/shard_map/all_to_all | solution.py:66
  75.6 7.3 %fusion.9 = f32[32,14,14,256]{3,0,2,1:T(8,128)} fusion(bf16[2304,256]{1,0:T(8,128)(2,1)S(1)} %bitcast.100, bf16[32,16,14,256]{3,0,2,1:T(8,128)(2,1)} %get-tuple-element.35, bf16[32,16,14,256]{3,0,2,1:T(8,128)(2,1)} %get-tuple-element.34, bf16[32,16,14,256]{3,0,2,1:T(8,128)(2,1)} %get-tuple-element.33), kind=kOutput, calls=%fused_computation.28 | convolution fusion | flops 2499280896 | bytes 17825792 | tf_op jit(solution)/shard_map/dot_general | solution.py:71
  85.0 5.4 %fusion.8 = f32[32,14,14,256]{3,0,2,1:T(8,128)} fusion(bf16[2304,256]{1,0:T(8,128)(2,1)S(1)} %bitcast.101, bf16[32,16,14,256]{3,0,2,1:T(8,128)(2,1)S(1)} %copy-done.2, bf16[32,16,14,256]{3,0,2,1:T(8,128)(2,1)S(1)} %copy-done.1, bf16[32,16,14,256]{3,0,2,1:T(8,128)(2,1)S(1)} %copy-done), kind=kOutput, calls=%fused_computation.26 | convolution fusion | flops 2499280896 | bytes 17825792 | tf_op jit(solution)/shard_map/dot_general | solution.py:71
  90.4 8.9 %multiply_reduce_fusion.1 = (f32[256]{0:T(256)S(1)}, f32[256]{0:T(256)S(1)}, f32[32,14,14,256]{3,0,2,1:T(8,128)}) fusion(bf16[2304,256]{1,0:T(8,128)(2,1)S(1)} %bitcast.102, bf16[32,16,14,256]{3,0,2,1:T(8,128)(2,1)S(1)} %copy-done.2, bf16[32,16,14,256]{3,0,2,1:T(8,128)(2,1)S(1)} %copy-done.1, bf16[32,16,14,256]{3,0,2,1:T(8,128)(2,1)S(1)} %copy-done, ...), kind=kOutput, calls=%fused_computation.5 | convolution fusion | flops 2507308544 | bytes 30672896 | tf_op jit(solution)/shard_map/dot_general | solution.py:71
  99.3 4.9 %all-reduce.5 = (f32[256]{0:T(256)S(1)}, f32[256]{0:T(256)S(1)}) all-reduce(f32[256]{0:T(256)S(1)} %get-tuple-element.10, f32[256]{0:T(256)S(1)} %get-tuple-element.9), channel_id=1, replica_groups=mesh['point'=32,'batch_0'=2,'batch_1'=2] {'batch_0'}, use_global_device_ids=true, to_apply=%region_8.9 | all-reduce | flops 512 | bytes 4096 | tf_op jit(solution)/shard_map/psum | solution.py:13
  104.2 2.4 %all-reduce.2 = (f32[256]{0:T(256)S(1)}, f32[256]{0:T(256)S(1)}) all-reduce(f32[256]{0:T(256)S(1)} %get-tuple-element.23, f32[256]{0:T(256)S(1)} %get-tuple-element.24), channel_id=1, replica_groups=mesh['point'=32,'batch_0'=2,'batch_1'=2] {'batch_1'}, use_global_device_ids=true, to_apply=%region_9.10 | all-reduce | flops 512 | bytes 4096 | tf_op jit(solution)/shard_map/psum | solution.py:13
  107.3 9.6 %all-to-all-start.3 = ((bf16[32,1000,32]{1,2,0:T(8,128)(2,1)}), bf16[32,1000,32]{1,2,0:T(8,128)(2,1)S(1)}, u32[]{:S(2)}, u32[]{:S(2)}) async-start(bf16[32,1000,32]{1,2,0:T(8,128)(2,1)} %add_convert_fusion), calls=%async_computation.3 | async-start | bytes 4194304 | tf_op jit(solution)/shard_map/all_to_all | solution.py:64
  116.9 14.0 %multiply_reduce_fusion = (f32[1024]{0:T(1024)S(1)}, f32[1024]{0:T(1024)S(1)}, f32[32,14,14,1024]{3,0,2,1:T(8,128)}) fusion(bf16[32,8,1024]{2,1,0:T(8,128)(2,1)S(1)} %all-to-all-done.2, f32[32,14,14,256]{3,0,2,1:T(8,128)} %get-tuple-element.64, f32[256]{0:T(256)S(1)} %bitcast.116, f32[256]{0:T(256)S(1)} %bitcast.117, f32[256]{0:T(256)S(1)} %get-tuple-element.29, ...), kind=kOutput, calls=%fused_computation.1 | convolution fusion | flops 3317233664 | bytes 32649216 | tf_op jit(solution)/shard_map/dot_general | solution.py:71
  130.9 5.0 %all-reduce.4 = (f32[1024]{0:T(1024)S(1)}, f32[1024]{0:T(1024)S(1)}) all-reduce(f32[1024]{0:T(1024)S(1)} %get-tuple-element.8, f32[1024]{0:T(1024)S(1)} %get-tuple-element.7), channel_id=1, replica_groups=mesh['point'=32,'batch_0'=2,'batch_1'=2] {'batch_0'}, use_global_device_ids=true, to_apply=%region_14.15 | all-reduce | flops 2048 | bytes 16384 | tf_op jit(solution)/shard_map/psum | solution.py:13
  135.9 2.5 %all-reduce.1 = (f32[1024]{0:T(1024)S(1)}, f32[1024]{0:T(1024)S(1)}) all-reduce(f32[1024]{0:T(1024)S(1)} %get-tuple-element.21, f32[1024]{0:T(1024)S(1)} %get-tuple-element.22), channel_id=1, replica_groups=mesh['point'=32,'batch_0'=2,'batch_1'=2] {'batch_1'}, use_global_device_ids=true, to_apply=%region_15.16 | all-reduce | flops 2048 | bytes 16384 | tf_op jit(solution)/shard_map/psum | solution.py:13
  139.0 14.7 %maximum_reduce_fusion = f32[32,1024]{1,0:T(8,128)S(1)} fusion(bf16[32,14,14,1024]{3,0,2,1:T(8,128)(2,1)} %param.11, f32[32,14,14,1024]{3,0,2,1:T(8,128)} %get-tuple-element.65, f32[1024]{0:T(1024)S(1)} %bitcast.106, f32[1024]{0:T(1024)S(1)} %bitcast.107, f32[1024]{0:T(1024)S(1)} %get-tuple-element.27, f32[1024]{0:T(1024)S(1)} %get-tuple-element.52), kind=kLoop, calls=%fused_computation | loop fusion | flops 51347456 | bytes 38682624 | tf_op jit(solution)/shard_map/reduce_sum | solution.py:145
  155.6 6.3 %all_to_all.54 = f32[4,1,1]{2,1,0:T(1,128)S(1)} all-to-all(f32[4,1,1]{2,1,0:T(1,128)S(1)} %broadcast_in_dim.46), channel_id=1, replica_groups=mesh['point'=32,'batch_0'=2,'batch_1'=2] {'batch_0','batch_1'}, dimensions={0} | all-to-all | bytes 32 | tf_op jit(solution)/shard_map/all_to_all | solution.py:19
  163.2 25.2 %all_to_all.55 = f32[32,1,1]{2,1,0:T(1,128)S(1)} all-to-all(f32[32,1,1]{2,1,0:T(1,128)S(1)} %broadcast_in_dim.47), channel_id=1, replica_groups=mesh['point'=32,'batch_0'=2,'batch_1'=2] {'point'}, dimensions={0} | all-to-all | bytes 256 | tf_op jit(solution)/shard_map/all_to_all | solution.py:19
  (42 shorter events, 14.1 us)
Async XLA Ops:
  3.3 24.6 %all-to-all-start = ((bf16[32,32,256]{2,1,0:T(8,128)(2,1)}), bf16[32,32,256]{2,1,0:T(8,128)(2,1)S(1)}, u32[]{:S(2)}, u32[]{:S(2)}) async-start(bf16[32,32,256]{2,1,0:T(8,128)(2,1)} %add_convert_fusion.3), calls=%async_computation | async-start | bytes 1048576 | tf_op jit(solution)/shard_map/all_to_all | solution.py:66
  27.9 37.8 %all-to-all-start.1 = ((bf16[32,72,256]{2,1,0:T(8,128)(2,1)}), bf16[32,72,256]{2,1,0:T(8,128)(2,1)S(1)}, u32[]{:S(2)}, u32[]{:S(2)}) async-start(bf16[32,72,256]{2,1,0:T(8,128)(2,1)} %add_convert_fusion.1), calls=%async_computation.1 | async-start | bytes 2359296 | tf_op jit(solution)/shard_map/all_to_all | solution.py:66
  56.8 9.0 %copy-start.4 = (f32[256]{0:T(256)}, f32[256]{0:T(256)S(1)}, u32[]{:S(2)}) copy-start(f32[256]{0:T(256)S(1)} %get-tuple-element.57) | copy-start | bytes 3076
  65.8 41.5 %all-to-all-start.2 = ((bf16[32,8,1024]{2,1,0:T(8,128)(2,1)}), bf16[32,8,1024]{2,1,0:T(8,128)(2,1)S(1)}, u32[]{:S(2)}, u32[]{:S(2)}) async-start(bf16[32,8,1024]{2,1,0:T(8,128)(2,1)} %add_convert_fusion.2), calls=%async_computation.2 | async-start | bytes 1048576 | tf_op jit(solution)/shard_map/all_to_all | solution.py:66
  75.6 7.3 %copy-start = (bf16[32,16,14,256]{3,0,2,1:T(8,128)(2,1)S(1)}, bf16[32,16,14,256]{3,0,2,1:T(8,128)(2,1)}, u32[]{:S(2)}) copy-start(bf16[32,16,14,256]{3,0,2,1:T(8,128)(2,1)} %get-tuple-element.33) | copy-start | bytes 11010052
  75.6 8.4 %copy-start.1 = (bf16[32,16,14,256]{3,0,2,1:T(8,128)(2,1)S(1)}, bf16[32,16,14,256]{3,0,2,1:T(8,128)(2,1)}, u32[]{:S(2)}) copy-start(bf16[32,16,14,256]{3,0,2,1:T(8,128)(2,1)} %get-tuple-element.34) | copy-start | bytes 11010052
  75.6 9.4 %copy-start.2 = (bf16[32,16,14,256]{3,0,2,1:T(8,128)(2,1)S(1)}, bf16[32,16,14,256]{3,0,2,1:T(8,128)(2,1)}, u32[]{:S(2)}) copy-start(bf16[32,16,14,256]{3,0,2,1:T(8,128)(2,1)} %get-tuple-element.35) | copy-start | bytes 11010052
  107.2 23.7 %copy-start.5 = (f32[256]{0:T(256)}, f32[256]{0:T(256)S(1)}, u32[]{:S(2)}) copy-start(f32[256]{0:T(256)S(1)} %get-tuple-element.56) | copy-start | bytes 3076
  107.3 46.5 %all-to-all-start.3 = ((bf16[32,1000,32]{1,2,0:T(8,128)(2,1)}), bf16[32,1000,32]{1,2,0:T(8,128)(2,1)S(1)}, u32[]{:S(2)}, u32[]{:S(2)}) async-start(bf16[32,1000,32]{1,2,0:T(8,128)(2,1)} %add_convert_fusion), calls=%async_computation.3 | async-start | bytes 4194304 | tf_op jit(solution)/shard_map/all_to_all | solution.py:64
  139.0 14.8 %copy-start.3 = (f32[1024]{0:T(1024)}, f32[1024]{0:T(1024)S(1)}, u32[]{:S(2)}) copy-start(f32[1024]{0:T(1024)S(1)} %get-tuple-element.52) | copy-start | bytes 12292
  139.0 14.8 %copy-start.6 = (s32[32]{0:T(128)S(1)}, s32[32]{0:T(128)}, u32[]{:S(2)}) copy-start(s32[32]{0:T(128)} %param.12) | copy-start | bytes 388
where the time goes:
time: 190 us; the launch traced here: 189 us
  blocking collectives  53.9 us (28%)
  matrix products  47.1 us (25%)
  starting transfers between devices  40 us (21%)
  other arithmetic  38.5 us (20%)
  local copies, waits for them, and re-layouts  8.33 us (4%)
    dot_general x5, matrix products, map_product(): lax.dot_general(maps, kernel, (((3,), (0,)), ((), ())), preferred_element...  46.5 us
    all_to_all x2, blocking collectives, sent_to_all(): return lax.all_to_all(copies, axis, split_axis=0, concat_axis=0, tiled=True)  31.5 us
    all_to_all x3, starting transfers between devices, point_weight(): lax.all_to_all(all_points, 'point', split_axis=0, concat_axis=1, tiled=True)  30.3 us
    psum x6, blocking collectives, by_axis(): x = lax.psum(x, axis)  22.4 us
    reduce_sum x1, other arithmetic, shards(): pooled = jnp.mean(block_out, axis=(1, 2)).astype(jnp.bfloat16)  14.7 us
    all_to_all x1, starting transfers between devices, point_weight(): lax.all_to_all(all_points, 'point', split_axis=0, concat_axis=2, tiled=True)  9.65 us
    convert_element_type x4, other arithmetic, point_weight(): all_points = blend_all(coefficients, endpoints).astype(jnp.bfloat16)  6.13 us
    add x2, other arithmetic, blend_all(): return start_part + bend_part + final_part  5.61 us
  transfers between devices with their start and end apart: 4, of which 0 were waited for; matrix products, arithmetic and copies ran while one was open for 45% of the time, Pallas kernels for 0%

commit v1 on v0

--- a/solution.py
+++ b/solution.py
@@ -10,7 +10,7 @@
 
 def by_axis(x, axes):
     for axis in axes:
-        x = lax.psum(x, axis)
+        x = lax.all_gather(x, axis).sum(axis=0)
     return x
 
 

time: 190 us -> 206 us (1.084)
  starting transfers between devices: 40 us -> 56.3 us
  blocking collectives: 53.9 us -> 42.9 us
  waiting for transfers between devices: 0.01 us -> 9.09 us
    all_gather x0 -> x12, blocking collectives: none -> 36.8 us  [by_axis(): x = lax.all_gather(x, axis).sum(axis=0)]
    all_to_all x2 -> x1, blocking collectives: 31.5 us -> 6.12 us  [sent_to_all(): return lax.all_to_all(copies, axis, split_axis=0, concat_axis=0, tiled=True)]
    psum x6 -> x0, blocking collectives: 22.4 us -> none  [by_axis(): x = lax.psum(x, axis)]
    all_to_all x0 -> x1, starting transfers between devices: none -> 16.1 us  [sent_to_all(): return lax.all_to_all(copies, axis, split_axis=0, concat_axis=0, tiled=True)]
    all_to_all x0 -> x1, waiting for transfers between devices: none -> 9.07 us  [sent_to_all(): return lax.all_to_all(copies, axis, split_axis=0, concat_axis=0, tiled=True)]
  transfers between devices with their start and end apart: 4 -> 5, of which waited for: 0 -> 1; matrix products, arithmetic and copies ran while one was open for 45% -> 42% of each run, Pallas kernels for 0% -> 0%
where the time goes in v1:
time: 206 us; the launch traced here: 205 us
  starting transfers between devices  56.3 us (27%)
  matrix products  47 us (23%)
  blocking collectives  42.9 us (21%)
  other arithmetic  38.7 us (19%)
  waiting for transfers between devices  9.09 us (4%)
  local copies, waits for them, and re-layouts  8.97 us (4%)
    dot_general x5, matrix products, map_product(): lax.dot_general(maps, kernel, (((3,), (0,)), ((), ())), preferred_element...  46.5 us
    all_gather x12, blocking collectives, by_axis(): x = lax.all_gather(x, axis).sum(axis=0)  36.8 us
    all_to_all x3, starting transfers between devices, point_weight(): lax.all_to_all(all_points, 'point', split_axis=0, concat_axis=1, tiled=True)  30.6 us
    all_to_all x1, starting transfers between devices, sent_to_all(): return lax.all_to_all(copies, axis, split_axis=0, concat_axis=0, tiled=True)  16.1 us
    reduce_sum x1, other arithmetic, shards(): pooled = jnp.mean(block_out, axis=(1, 2)).astype(jnp.bfloat16)  14.7 us
    all_to_all x1, starting transfers between devices, point_weight(): lax.all_to_all(all_points, 'point', split_axis=0, concat_axis=2, tiled=True)  9.67 us
    all_to_all x1, waiting for transfers between devices, sent_to_all(): return lax.all_to_all(copies, axis, split_axis=0, concat_axis=0, tiled=True)  9.07 us
    convert_element_type x4, other arithmetic, point_weight(): all_points = blend_all(coefficients, endpoints).astype(jnp.bfloat16)  6.13 us
  transfers between devices with their start and end apart: 5, of which 1 were waited for; matrix products, arithmetic and copies ran while one was open for 42% of the time, Pallas kernels for 0%

profile of v1, /device:TPU:0, one launch (start us, length us, event | category | flops | bytes accessed | tf_op | source)
XLA Modules:
  0.0 204.5 jit_solution(147930060812155955)
XLA Ops:
  3.3 10.7 %all-to-all-start = ((bf16[32,32,256]{2,1,0:T(8,128)(2,1)}), bf16[32,32,256]{2,1,0:T(8,128)(2,1)S(1)}, u32[]{:S(2)}, u32[]{:S(2)}) async-start(bf16[32,32,256]{2,1,0:T(8,128)(2,1)} %add_convert_fusion.3), calls=%async_computation | async-start | bytes 1048576 | tf_op jit(solution)/shard_map/all_to_all | solution.py:66
  14.7 2.8 %multiply_add_fusion = (f32[1,1536]{1,0:T(1,128)S(1)}, f32[1,1536]{1,0:T(1,128)S(1)}) fusion(f32[3,1536]{1,0:T(4,128)} %param.20, f32[]{:T(128)} %bitcast.17, f32[]{:T(128)} %bitcast.16, f32[]{:T(128)} %bitcast.15, f32[3,1536]{1,0:T(4,128)} %param.19), kind=kLoop, calls=%fused_computation.48 | loop fusion | flops 15360 | bytes 49164 | tf_op jit(solution)/shard_map/add | solution.py:58
  19.1 2.8 %multiply_add_fusion.2 = f32[1,1000]{1,0:T(1,128)S(1)} fusion(f32[3,1000]{1,0:T(4,128)} %param.21, f32[]{:T(128)} %bitcast.17, f32[]{:T(128)} %bitcast.16, f32[]{:T(128)} %bitcast.15), kind=kLoop, calls=%fused_computation.50 | loop fusion | flops 5000 | bytes 16012 | tf_op jit(solution)/shard_map/add | solution.py:58
  25.6 2.4 %add_convert_fusion = bf16[32,1000,32]{1,2,0:T(8,128)(2,1)} fusion(f32[1000,32]{0,1:T(8,128)S(1)} %get-tuple-element.19, f32[32]{0:T(128)S(1)} %get-tuple-element.48, f32[1000,32]{0,1:T(8,128)S(1)} %get-tuple-element.20, f32[32]{0:T(128)S(1)} %get-tuple-element.49, f32[1000,32]{0,1:T(8,128)S(1)} %get-tuple-element.18, f32[32]{0:T(128)S(1)} %get-tuple-element.50), kind=kLoop, calls=%fused_computation.8 | loop fusion | flops 6144000 | bytes 2432384 | tf_op jit(solution)/shard_map/convert_element_type | solution.py:62
  27.9 9.8 %all-to-all-start.1 = ((bf16[32,72,256]{2,1,0:T(8,128)(2,1)}), bf16[32,72,256]{2,1,0:T(8,128)(2,1)S(1)}, u32[]{:S(2)}, u32[]{:S(2)}) async-start(bf16[32,72,256]{2,1,0:T(8,128)(2,1)} %add_convert_fusion.1), calls=%async_computation.1 | async-start | bytes 2359296 | tf_op jit(solution)/shard_map/all_to_all | solution.py:66
  37.8 10.8 %multiply_reduce_fusion.2 = (f32[256]{0:T(256)S(1)}, f32[256]{0:T(256)S(1)}, f32[256,32,14,14]{0,1,3,2:T(8,128)}) fusion(bf16[1024,256,1,1]{1,0,3,2:T(8,128)(2,1)S(1)} %bitcast.111, bf16[32,14,14,1024]{3,0,2,1:T(8,128)(2,1)} %param.11), kind=kOutput, calls=%fused_computation.7 | convolution fusion | flops 3293150720 | bytes 19793920 | tf_op jit(solution)/shard_map/dot_general | solution.py:71
  48.6 4.2 %all-gather.12 = f32[2,1,256]{2,1,0:T(1,128)S(1)} all-gather(f32[1,1,256]{2,1,0:T(1,128)S(1)} %bitcast.134), channel_id=2, replica_groups=mesh['point'=32,'batch_0'=2,'batch_1'=2] {'batch_0'}, dimensions={0}, use_global_device_ids=true | all-gather | bytes 3072 | tf_op jit(solution)/shard_map/all_gather | solution.py:13
  54.7 4.2 %all-gather.14 = f32[2,1,256]{2,1,0:T(1,128)S(1)} all-gather(f32[1,1,256]{2,1,0:T(1,128)S(1)} %bitcast.132), channel_id=4, replica_groups=mesh['point'=32,'batch_0'=2,'batch_1'=2] {'batch_0'}, dimensions={0}, use_global_device_ids=true | all-gather | bytes 3072 | tf_op jit(solution)/shard_map/all_gather | solution.py:13
  61.4 4.1 %fusion.1 = bf16[32,14,14,256]{3,0,2,1:T(8,128)(2,1)S(1)} fusion(f32[256,32,14,14]{0,1,3,2:T(8,128)} %get-tuple-element.51, f32[256]{0:T(256)S(1)} %bitcast.121, f32[256]{0:T(256)S(1)} %bitcast.122, f32[256]{0:T(256)S(1)} %get-tuple-element.43, f32[256]{0:T(256)S(1)} %get-tuple-element.45), kind=kLoop, calls=%fused_computation.13 | loop fusion | flops 9633792 | bytes 9637888 | tf_op jit(solution)/shard_map/convert_element_type | solution.py:134
  65.4 4.9 %pad_slice_fusion.2 = (bf16[32,16,14,256]{3,0,2,1:T(8,128)(2,1)}, bf16[32,16,14,256]{3,0,2,1:T(8,128)(2,1)}, bf16[32,16,14,256]{3,0,2,1:T(8,128)(2,1)}) fusion(bf16[32,14,14,256]{3,0,2,1:T(8,128)(2,1)S(1)} %fusion.1), kind=kLoop, calls=%fused_computation.11 | loop fusion | bytes 14221312 | tf_op jit(solution)/shard_map/slice | solution.py:93
  70.4 10.0 %all-to-all-start.2 = ((bf16[32,8,1024]{2,1,0:T(8,128)(2,1)}), bf16[32,8,1024]{2,1,0:T(8,128)(2,1)S(1)}, u32[]{:S(2)}, u32[]{:S(2)}) async-start(bf16[32,8,1024]{2,1,0:T(8,128)(2,1)} %add_convert_fusion.2), calls=%async_computation.2 | async-start | bytes 1048576 | tf_op jit(solution)/shard_map/all_to_all | solution.py:66
  80.4 7.3 %fusion.9 = f32[32,14,14,256]{3,0,2,1:T(8,128)} fusion(bf16[2304,256]{1,0:T(8,128)(2,1)S(1)} %bitcast.108, bf16[32,16,14,256]{3,0,2,1:T(8,128)(2,1)} %get-tuple-element.17, bf16[32,16,14,256]{3,0,2,1:T(8,128)(2,1)} %get-tuple-element.16, bf16[32,16,14,256]{3,0,2,1:T(8,128)(2,1)} %get-tuple-element.15), kind=kOutput, calls=%fused_computation.28 | convolution fusion | flops 2499280896 | bytes 17825792 | tf_op jit(solution)/shard_map/dot_general | solution.py:71
  89.8 5.4 %fusion.8 = f32[32,14,14,256]{3,0,2,1:T(8,128)} fusion(bf16[2304,256]{1,0:T(8,128)(2,1)S(1)} %bitcast.109, bf16[32,16,14,256]{3,0,2,1:T(8,128)(2,1)S(1)} %copy-done.2, bf16[32,16,14,256]{3,0,2,1:T(8,128)(2,1)S(1)} %copy-done.1, bf16[32,16,14,256]{3,0,2,1:T(8,128)(2,1)S(1)} %copy-done), kind=kOutput, calls=%fused_computation.26 | convolution fusion | flops 2499280896 | bytes 17825792 | tf_op jit(solution)/shard_map/dot_general | solution.py:71
  95.2 8.9 %multiply_reduce_fusion.1 = (f32[256]{0:T(256)S(1)}, f32[256]{0:T(256)S(1)}, f32[32,14,14,256]{3,0,2,1:T(8,128)}) fusion(bf16[2304,256]{1,0:T(8,128)(2,1)S(1)} %bitcast.110, bf16[32,16,14,256]{3,0,2,1:T(8,128)(2,1)S(1)} %copy-done.2, bf16[32,16,14,256]{3,0,2,1:T(8,128)(2,1)S(1)} %copy-done.1, bf16[32,16,14,256]{3,0,2,1:T(8,128)(2,1)S(1)} %copy-done, ...), kind=kOutput, calls=%fused_computation.5 | convolution fusion | flops 2507308544 | bytes 30672896 | tf_op jit(solution)/shard_map/dot_general | solution.py:71
  104.1 4.2 %all-gather.16 = f32[2,1,256]{2,1,0:T(1,128)S(1)} all-gather(f32[1,1,256]{2,1,0:T(1,128)S(1)} %bitcast.133), channel_id=6, replica_groups=mesh['point'=32,'batch_0'=2,'batch_1'=2] {'batch_0'}, dimensions={0}, use_global_device_ids=true | all-gather | bytes 3072 | tf_op jit(solution)/shard_map/all_gather | solution.py:13
  110.2 4.2 %all-gather.18 = f32[2,1,256]{2,1,0:T(1,128)S(1)} all-gather(f32[1,1,256]{2,1,0:T(1,128)S(1)} %bitcast.131), channel_id=8, replica_groups=mesh['point'=32,'batch_0'=2,'batch_1'=2] {'batch_0'}, dimensions={0}, use_global_device_ids=true | all-gather | bytes 3072 | tf_op jit(solution)/shard_map/all_gather | solution.py:13
  116.3 9.7 %all-to-all-start.3 = ((bf16[32,1000,32]{1,2,0:T(8,128)(2,1)}), bf16[32,1000,32]{1,2,0:T(8,128)(2,1)S(1)}, u32[]{:S(2)}, u32[]{:S(2)}) async-start(bf16[32,1000,32]{1,2,0:T(8,128)(2,1)} %add_convert_fusion), calls=%async_computation.3 | async-start | bytes 4194304 | tf_op jit(solution)/shard_map/all_to_all | solution.py:64
  126.0 14.0 %multiply_reduce_fusion = (f32[1024]{0:T(1024)S(1)}, f32[1024]{0:T(1024)S(1)}, f32[32,14,14,1024]{3,0,2,1:T(8,128)}) fusion(bf16[32,8,1024]{2,1,0:T(8,128)(2,1)S(1)} %all-to-all-done.2, f32[32,14,14,256]{3,0,2,1:T(8,128)} %get-tuple-element.52, f32[256]{0:T(256)S(1)} %bitcast.135, f32[256]{0:T(256)S(1)} %bitcast.136, f32[256]{0:T(256)S(1)} %get-tuple-element.40, ...), kind=kOutput, calls=%fused_computation.1 | convolution fusion | flops 3317233664 | bytes 32649216 | tf_op jit(solution)/shard_map/dot_general | solution.py:71
  140.0 4.4 %all-gather.8 = f32[2048]{0:T(1024)S(1)} all-gather(f32[1024]{0:T(1024)S(1)} %get-tuple-element.8), channel_id=10, replica_groups=mesh['point'=32,'batch_0'=2,'batch_1'=2] {'batch_0'}, dimensions={0}, use_global_device_ids=true | all-gather | bytes 12288 | tf_op jit(solution)/shard_map/all_gather | solution.py:13
  146.3 4.6 %all-gather.10 = f32[2048]{0:T(1024)S(1)} all-gather(f32[1024]{0:T(1024)S(1)} %get-tuple-element.7), channel_id=12, replica_groups=mesh['point'=32,'batch_0'=2,'batch_1'=2] {'batch_0'}, dimensions={0}, use_global_device_ids=true | all-gather | bytes 12288 | tf_op jit(solution)/shard_map/all_gather | solution.py:13
  153.4 14.7 %maximum_reduce_fusion = f32[32,1024]{1,0:T(8,128)S(1)} fusion(bf16[32,14,14,1024]{3,0,2,1:T(8,128)(2,1)} %param.11, f32[32,14,14,1024]{3,0,2,1:T(8,128)} %get-tuple-element.53, f32[1024]{0:T(1024)S(1)} %bitcast.115, f32[1024]{0:T(1024)S(1)} %bitcast.116, f32[1024]{0:T(1024)S(1)} %get-tuple-element.34, f32[1024]{0:T(1024)S(1)} %get-tuple-element.36), kind=kLoop, calls=%fused_computation | loop fusion | flops 51347456 | bytes 38682624 | tf_op jit(solution)/shard_map/reduce_sum | solution.py:145
  170.0 6.1 %all_to_all.54 = f32[4,1,1]{2,1,0:T(1,128)S(1)} all-to-all(f32[4,1,1]{2,1,0:T(1,128)S(1)} %broadcast_in_dim.26), channel_id=1, replica_groups=mesh['point'=32,'batch_0'=2,'batch_1'=2] {'batch_0','batch_1'}, dimensions={0} | all-to-all | bytes 32 | tf_op jit(solution)/shard_map/all_to_all | solution.py:19
  178.0 16.1 %all-to-all-start.5 = ((f32[32,1,1]{2,1,0:T(1,128)}), f32[32,1,1]{2,1,0:T(1,128)S(1)}, u32[]{:S(2)}, u32[]{:S(2)}) async-start(f32[32,1,1]{2,1,0:T(1,128)} %broadcast_in_dim.27), calls=%async_computation.5 | async-start | bytes 32768 | tf_op jit(solution)/shard_map/all_to_all | solution.py:19
  194.6 9.1 %all-to-all-done.5 = f32[32,1,1]{2,1,0:T(1,128)S(1)} async-done(((f32[32,1,1]{2,1,0:T(1,128)}), f32[32,1,1]{2,1,0:T(1,128)S(1)}, u32[]{:S(2)}, u32[]{:S(2)}) %all-to-all-start.5) | async-done | bytes 160 | tf_op jit(solution)/shard_map/all_to_all | solution.py:19
  (68 shorter events, 27.4 us)
Async XLA Ops:
  3.3 24.6 %all-to-all-start = ((bf16[32,32,256]{2,1,0:T(8,128)(2,1)}), bf16[32,32,256]{2,1,0:T(8,128)(2,1)S(1)}, u32[]{:S(2)}, u32[]{:S(2)}) async-start(bf16[32,32,256]{2,1,0:T(8,128)(2,1)} %add_convert_fusion.3), calls=%async_computation | async-start | bytes 1048576 | tf_op jit(solution)/shard_map/all_to_all | solution.py:66
  27.9 42.4 %all-to-all-start.1 = ((bf16[32,72,256]{2,1,0:T(8,128)(2,1)}), bf16[32,72,256]{2,1,0:T(8,128)(2,1)S(1)}, u32[]{:S(2)}, u32[]{:S(2)}) async-start(bf16[32,72,256]{2,1,0:T(8,128)(2,1)} %add_convert_fusion.1), calls=%async_computation.1 | async-start | bytes 2359296 | tf_op jit(solution)/shard_map/all_to_all | solution.py:66
  60.8 9.6 %copy-start.4 = (f32[256]{0:T(256)}, f32[256]{0:T(256)S(1)}, u32[]{:S(2)}) copy-start(f32[256]{0:T(256)S(1)} %get-tuple-element.45) | copy-start | bytes 3076
  70.4 45.9 %all-to-all-start.2 = ((bf16[32,8,1024]{2,1,0:T(8,128)(2,1)}), bf16[32,8,1024]{2,1,0:T(8,128)(2,1)S(1)}, u32[]{:S(2)}, u32[]{:S(2)}) async-start(bf16[32,8,1024]{2,1,0:T(8,128)(2,1)} %add_convert_fusion.2), calls=%async_computation.2 | async-start | bytes 1048576 | tf_op jit(solution)/shard_map/all_to_all | solution.py:66
  80.4 7.3 %copy-start = (bf16[32,16,14,256]{3,0,2,1:T(8,128)(2,1)S(1)}, bf16[32,16,14,256]{3,0,2,1:T(8,128)(2,1)}, u32[]{:S(2)}) copy-start(bf16[32,16,14,256]{3,0,2,1:T(8,128)(2,1)} %get-tuple-element.15) | copy-start | bytes 11010052
  80.4 8.4 %copy-start.1 = (bf16[32,16,14,256]{3,0,2,1:T(8,128)(2,1)S(1)}, bf16[32,16,14,256]{3,0,2,1:T(8,128)(2,1)}, u32[]{:S(2)}) copy-start(bf16[32,16,14,256]{3,0,2,1:T(8,128)(2,1)} %get-tuple-element.16) | copy-start | bytes 11010052
  80.4 9.4 %copy-start.2 = (bf16[32,16,14,256]{3,0,2,1:T(8,128)(2,1)S(1)}, bf16[32,16,14,256]{3,0,2,1:T(8,128)(2,1)}, u32[]{:S(2)}) copy-start(bf16[32,16,14,256]{3,0,2,1:T(8,128)(2,1)} %get-tuple-element.17) | copy-start | bytes 11010052
  116.3 77.8 %copy-start.5 = (f32[256]{0:T(256)}, f32[256]{0:T(256)S(1)}, u32[]{:S(2)}) copy-start(f32[256]{0:T(256)S(1)} %get-tuple-element.42) | copy-start | bytes 3076
  116.3 51.8 %all-to-all-start.3 = ((bf16[32,1000,32]{1,2,0:T(8,128)(2,1)}), bf16[32,1000,32]{1,2,0:T(8,128)(2,1)S(1)}, u32[]{:S(2)}, u32[]{:S(2)}) async-start(bf16[32,1000,32]{1,2,0:T(8,128)(2,1)} %add_convert_fusion), calls=%async_computation.3 | async-start | bytes 4194304 | tf_op jit(solution)/shard_map/all_to_all | solution.py:64
  152.8 15.4 %copy-start.3 = (f32[1024]{0:T(1024)}, f32[1024]{0:T(1024)S(1)}, u32[]{:S(2)}) copy-start(f32[1024]{0:T(1024)S(1)} %get-tuple-element.36) | copy-start | bytes 12292
  153.4 14.8 %copy-start.6 = (s32[32]{0:T(128)S(1)}, s32[32]{0:T(128)}, u32[]{:S(2)}) copy-start(s32[32]{0:T(128)} %param.12) | copy-start | bytes 388
  178.0 25.7 %all-to-all-start.5 = ((f32[32,1,1]{2,1,0:T(1,128)}), f32[32,1,1]{2,1,0:T(1,128)S(1)}, u32[]{:S(2)}, u32[]{:S(2)}) async-start(f32[32,1,1]{2,1,0:T(1,128)} %broadcast_in_dim.27), calls=%async_computation.5 | async-start | bytes 32768 | tf_op jit(solution)/shard_map/all_to_all | solution.py:19
